TPU v7x, 32 devices: a whole 2x2x4 slice. The times are simulated.
32 devices in a mesh: row: 16 (over z, y, x), col: 2 (over core).
Axes of the slice: x: 2, y: 2, z: 4, core: 2. Of those that a mesh axis runs over, the one named last changes fastest.
Arguments:
- inv_diag: float32 [16, 1088, 1088], P('row', None, 'col'), may hold values from -0.1875 to 0.1875
- low_left: float32 [16, 1088, 96], P('row', 'col'), may hold values from -0.1875 to 0.1875
- low_right: float32 [16, 1088, 96], P('row', 'col'), may hold values from -0.625 to 0.625
- deriv_diag: bfloat16 [3, 16, 1088, 1088], P(None, 'row', None, 'col'), may hold values from -0.1875 to 0.1875
- deriv_left: float32 [3, 16, 1088, 96], P(None, 'row', 'col'), may hold values from -0.1875 to 0.1875
- deriv_right: float32 [3, 16, 1088, 96], P(None, 'row', 'col'), may hold values from -0.625 to 0.625
- ranks: int32 [4, 16], P(None, 'row'), may hold values from 88 to 96
- whitened: float32 [17408], P(('row', 'col')), may hold values from -6 to 6
- probes: int32 [8, 17408], P(None, ('row', 'col')), may hold values from -1 to 1, as said below
Outputs:
- solved: float32 [9, 17408], P(None, ('row', 'col'))
- whitened_deriv: float32 [3, 8, 17408], P(None, None, ('row', 'col'))
- fisher: float32 [3, 3], replicated
- score: float32 [3], replicated
Inputs may be any that keep to these rules, and one draw needn't show every extreme that they name: `probes`: every entry is -1 or +1. `ranks`: column 0 belongs to no tile.
All inputs are finite; a program needn't handle non-finite values.
Results may differ from a plain program's by a relative error of at most 0.0019.
Values sent between devices are 32-bit elements; how exact they have to be, the bound alone decides.
A program may use at most 64 MiB of HBM per device.

v0:
```python
import functools

import jax
import jax.numpy as jnp
from jax import lax
from jax.experimental import pallas as pl
from jax.experimental.pallas import tpu as pltpu
from jax.sharding import PartitionSpec as P

f32, bf16 = jnp.float32, jnp.bfloat16
MESH = pl.DeviceIdType.MESH
NN = (((1,), (0,)), ((), ()))
NT = (((1,), (1,)), ((), ()))


def split(x):
    high = x.astype(bf16)
    return high, (x - high.astype(f32)).astype(bf16)


def dot1(a, b, dims):
    return lax.dot_general(a, b, dims, preferred_element_type=f32)


def dot3(a, b, dims):
    return dot1(a[0], b[0], dims) + (dot1(a[0], b[1], dims) + dot1(a[1], b[0], dims))


def mul(a, b, dims=NN):
    return dot3(split(a), split(b), dims)


def group_size(rows):
    return max(d for d in range(1, rows + 1) if rows % d == 0 and d * d <= rows)


def kernel(
    rows, q_hbm, u_hbm, v_hbm, d_hbm, du_hbm, dv_hbm, ranks_hbm, white_hbm, probes_hbm,
    solved_ref, deriv_ref, fisher_ref, score_ref,
    ranks_ref, white_ref, probes_ref, q, u, own_v, d, du, dv, q_high, q_low, v_all, src_all,
    du_high, du_low, dv_high, dv_low,
    m_part, m_other, m_all, lin_all, off_all, x_own, x_prior, up_part, up_other, up_send, up_recv,
    dense_send, dense_recv, low_part, low_other, s_part, s_other, s_all, o_all,
    w_send, w_recv, tot_all,
    load_sem, pair_send, pair_recv, row_send, row_recv,
    g1_send, g1_recv, l_send, l_recv, g2_send, g2_recv, g3_send, g3_recv, g4_send, g4_recv, tot_send, tot_recv,
):
    i, c = lax.axis_index("row"), lax.axis_index("col")
    p = 1 - c
    half, size = q.shape
    rmax = u.shape[0]
    params = d.shape[0]
    count = s_part.shape[0] // params
    pad = src_all.shape[1]
    group = m_all.shape[0]
    groups = lin_all.shape[0]
    g, l = i // group, i % group

    loads = [
        pltpu.make_async_copy(u_hbm.at[0], u, load_sem.at[0]),
        pltpu.make_async_copy(q_hbm.at[0], q, load_sem.at[1]),
        pltpu.make_async_copy(du_hbm.at[:, 0], du, load_sem.at[2]),
        pltpu.make_async_copy(dv_hbm.at[:, 0], dv, load_sem.at[3]),
        pltpu.make_async_copy(d_hbm.at[:, 0], d, load_sem.at[4]),
    ]
    own_v_load = pltpu.make_async_copy(v_hbm.at[0], own_v, load_sem.at[5])
    small_loads = [
        pltpu.make_async_copy(probes_hbm, probes_ref, load_sem.at[6]),
        pltpu.make_async_copy(white_hbm, white_ref, load_sem.at[7]),
        pltpu.make_async_copy(ranks_hbm, ranks_ref, load_sem.at[8]),
    ]
    own_v_load.start()
    for load in small_loads:
        load.start()
    for load in loads:
        load.start()

    barrier = pltpu.get_barrier_semaphore()

    def greet(k, carry):
        row = lax.rem(i + k, rows)
        for col in range(2):
            @pl.when(jnp.logical_or(k > 0, col != c))
            def _():
                pl.semaphore_signal(barrier, inc=1, device_id=(row, col), device_id_type=MESH)
        return carry

    lax.fori_loop(0, rows, greet, 0)
    pl.semaphore_wait(barrier, 2 * rows - 1)

    def pair(k, src, dst):
        return pltpu.make_async_remote_copy(
            src_ref=src, dst_ref=dst, send_sem=pair_send.at[k], recv_sem=pair_recv.at[k],
            device_id=(i, p), device_id_type=MESH,
        )

    def hop(k, src, dst, distance):
        return pltpu.make_async_remote_copy(
            src_ref=src, dst_ref=dst, send_sem=row_send.at[k], recv_sem=row_recv.at[k],
            device_id=(lax.rem(i + distance + rows, rows), c), device_id_type=MESH,
        )

    own_v_load.wait()
    v_hop = hop(0, own_v, v_all.at[c], -1)

    @pl.when(i > 0)
    def _():
        v_hop.start()

    for load in small_loads:
        load.wait()
    signs = probes_ref[...].astype(f32)
    src_own = jnp.concatenate(
        [signs, white_ref[...].reshape(1, half), jnp.zeros((pad - count - 1, half), f32)], axis=0
    )
    src_all[c] = src_own
    src_pair = pair(0, src_all.at[c], src_all.at[c])
    src_pair.start()

    lane_of = lax.broadcasted_iota(jnp.int32, (1, rmax), 1)
    row_of = lax.broadcasted_iota(jnp.int32, (rmax, 1), 0)
    masks = [(lane_of < ranks_ref[:, k:k + 1]).astype(f32) for k in range(params + 1)]
    loads[0].wait()
    u[...] = u[...] * (row_of < ranks_ref[:, 0:1]).astype(f32)
    u_split = split(u[...])
    loads[1].wait()
    q_high[...], q_low[...] = split(q[...])

    v_pair = pair(1, v_all.at[c], v_all.at[c])

    @pl.when(i < rows - 1)
    def _():
        v_hop.wait_recv()

    @pl.when(i == rows - 1)
    def _():
        v_all[c] = jnp.zeros((rmax, half), f32)

    v_pair.start()
    src_pair.wait_recv()
    v_pair.wait_recv()

    halves = [jnp.concatenate([v_all[s], src_all[s]], axis=0) for s in range(2)]
    both = dot3(split(jnp.concatenate(halves, axis=1)), (q_high[...], q_low[...]), NT)
    wide_t, base = both[:rmax], both[rmax:]
    wide_split = split(wide_t)
    m_part[...] = dot3(split(both), u_split, NT)
    m_pair = pair(2, m_part, m_other)
    m_pair.start()
    m_pair.wait_recv()
    m_own = m_part[...] + m_other[...]
    m_all[l] = m_own

    def spread(block, mine, send, recv, span, device):
        copies = []
        for k in range(1, span):
            copies.append(pltpu.make_async_remote_copy(
                src_ref=block.at[mine], dst_ref=block.at[mine],
                send_sem=send.at[k], recv_sem=recv.at[k],
                device_id=(device(lax.rem(mine + k, span)), c), device_id_type=MESH,
            ))
        for copy in copies:
            copy.start()
        return copies

    in_group = lambda member: g * group + member
    across = lambda other: other * group + l

    g1 = spread(m_all, l, g1_send, g1_recv, group, in_group)
    for load in loads[2:4]:
        load.wait()
    for k in range(params):
        du_high[k], du_low[k] = split(du[k])
        dv_high[k], dv_low[k] = split(dv[k])
    for copy in g1:
        copy.wait_recv()
    m_split = [split(m_all[m, :rmax]) for m in range(group)]
    lift = [m_all[m, rmax:] for m in range(group)]
    lin, off = -m_all[group - 1, :rmax], lift[group - 1]
    for m in reversed(range(group - 1)):
        state = dot3(split(jnp.concatenate([lin, off], axis=0)), m_split[m], NN)
        lin, off = -state[:rmax], lift[m] - state[rmax:]
    lin_all[g] = lin
    off_all[g] = off

    def to_groups(block, send, recv):
        return [
            pltpu.make_async_remote_copy(
                src_ref=block.at[g], dst_ref=block.at[g],
                send_sem=send.at[m], recv_sem=recv.at[g],
                device_id=(across(m), c), device_id_type=MESH,
            )
            for m in range(groups)
        ]

    def from_group(block, recv, m):
        return pltpu.make_async_remote_copy(
            src_ref=block.at[m], dst_ref=block.at[m],
            send_sem=recv.at[m], recv_sem=recv.at[m],
            device_id=(across(m), c), device_id_type=MESH,
        )

    def when_each(test, act, items):
        for m, item in enumerate(items):
            @pl.when(test(m))
            def _():
                act(item)

    everyone = list(range(groups))
    inner = jnp.logical_and(g > 0, g < groups - 1)
    lin_copies = to_groups(lin_all, l_send, l_recv)
    off_copies = to_groups(off_all, g2_send, g2_recv)
    when_each(lambda m: m < g, lambda copy: copy.start(), off_copies)
    when_each(lambda m: jnp.logical_and(inner, m != g), lambda copy: copy.start(), lin_copies)
    when_each(lambda m: m > g, lambda m: from_group(off_all, g2_recv, m).wait_recv(), everyone)
    for m in range(1, groups - 1):
        @pl.when(m != g)
        def _():
            from_group(lin_all, l_recv, m).wait_recv()
    t_split = [split(lin_all[m]) for m in range(groups)]
    a = jnp.zeros((pad, rmax), f32)
    for m in reversed(range(1, groups)):
        new = off_all[m]
        if m < groups - 1:
            new = new + dot3(split(a), t_split[m], NN)
        a = jnp.where(m > g, new, a)
    for m in reversed(range(1, group)):
        a = jnp.where(m > l, lift[m] - dot3(split(a), m_split[m], NN), a)

    x = base - dot3(split(a), wide_split, NN)
    x_own[...] = x
    x_hop = hop(1, x_own, x_prior, 1)

    @pl.when(i < rows - 1)
    def _():
        x_hop.start()

    x_split = split(x)
    du_split = [(du_high[k], du_low[k]) for k in range(params)]
    dv_split = [(dv_high[k], dv_low[k]) for k in range(params)]
    for k in range(params):
        up_part[k] = dot3(x_split, du_split[k], NT)
    up_pair = pair(3, up_part, up_other)
    up_pair.start()
    solved_ref[0:1] = x[count:count + 1]
    solved_ref[1:] = x[:count]
    rounded = x_split[0]
    loads[4].wait()

    def pack(ref, k, block):
        ref[k * count:(k + 1) * count] = block[:count]
        ref[params * count + k:params * count + k + 1] = block[count:count + 1]

    def halves_of(block):
        low, high = block[:, :half], block[:, half:]
        return jnp.where(c == 0, low, high), jnp.where(c == 0, high, low)

    dense = [halves_of(dot1(rounded, d[k], NN)) for k in range(params)]
    for k in range(params):
        pack(dense_send, k, dense[k][1])
    dense_pair = pair(4, dense_send, dense_recv)
    dense_pair.start()
    up_pair.wait_recv()
    for k in range(params):
        coeff = (up_part[k] + up_other[k]) * masks[k + 1]
        pack(up_send, k, dot3(split(coeff), dv_split[k], NN))
    up_hop = hop(2, up_send, up_recv, -1)

    @pl.when(i > 0)
    def _():
        up_hop.start()

    @pl.when(i > 0)
    def _():
        x_hop.wait_recv()

    @pl.when(i == 0)
    def _():
        x_prior[...] = jnp.zeros((pad, half), f32)

    prior_split = split(x_prior[...])
    for k in range(params):
        low_part[k] = dot3(prior_split, dv_split[k], NT)
    low_pair = pair(5, low_part, low_other)
    low_pair.start()
    low_pair.wait_recv()
    lower = []
    for k in range(params):
        coeff = (low_part[k] + low_other[k]) * masks[k + 1]
        lower.append(dense[k][0] + dot3(split(coeff), du_split[k], NN))
    dense_pair.wait_recv()

    @pl.when(i < rows - 1)
    def _():
        up_hop.wait_recv()

    @pl.when(i == rows - 1)
    def _():
        up_recv[...] = jnp.zeros(up_recv.shape, f32)

    other = dense_recv[...] + up_recv[...]
    drive = jnp.concatenate([part[:count] for part in lower], axis=0) + other[:params * count]
    observed = [
        lower[k][count:count + 1] + other[params * count + k:params * count + k + 1]
        for k in range(params)
    ]
    s_part[...] = dot3(split(drive), wide_split, NT)
    s_pair = pair(6, s_part, s_other)
    s_pair.start()
    s_pair.wait_recv()
    s_all[l] = s_part[...] + s_other[...]
    g3 = spread(s_all, l, g3_send, g3_recv, group, in_group)
    for copy in g3:
        copy.wait_recv()
    total = s_all[0]
    for m in range(1, group):
        total = s_all[m] - dot3(split(total), m_split[m], NT)
    o_all[g] = total
    o_copies = to_groups(o_all, g4_send, g4_recv)
    when_each(lambda m: m > g, lambda copy: copy.start(), o_copies)
    when_each(lambda m: m < g, lambda m: from_group(o_all, g4_recv, m).wait_recv(), everyone)
    b = jnp.zeros((params * count, rmax), f32)
    for m in range(groups - 1):
        new = o_all[m]
        if m > 0:
            new = new + dot3(split(b), t_split[m], NT)
        b = jnp.where(m < g, new, b)
    for m in range(group - 1):
        b = jnp.where(m < l, s_all[m] - dot3(split(b), m_split[m], NT), b)

    rest = split(drive - dot3(split(b), u_split, NN))
    w, w_send[...] = halves_of(dot3(rest, (q_high[...], q_low[...]), NN))
    w_pair = pair(7, w_send, w_recv)
    w_pair.start()
    w_pair.wait_recv()
    w = w + w_recv[...]
    parts = [w[k * count:(k + 1) * count] for k in range(params)]
    for k in range(params):
        deriv_ref[k] = parts[k]

    lanes = tot_all.shape[2]
    lane = lax.broadcasted_iota(jnp.int32, (1, lanes), 1)
    packed = jnp.zeros((1, lanes), f32)

    def put(packed, at, value):
        summed = jnp.sum(jnp.sum(value, axis=0, keepdims=True), axis=1, keepdims=True)
        return jnp.where(lane == at, summed, packed)

    for k in range(params):
        for m in range(k, params):
            product = parts[k] * parts[m]
            packed = put(packed, k * params + m, product)
        packed = put(packed, params * params + k, parts[k] * signs)
        data = observed[k] * x[count:count + 1]
        packed = put(packed, params * params + params + k, data)
    me = 2 * i + c
    devices = 2 * rows
    tot_all[me] = packed

    def tot_copy(k):
        other = lax.rem(me + k, devices)
        return pltpu.make_async_remote_copy(
            src_ref=tot_all.at[me], dst_ref=tot_all.at[me],
            send_sem=tot_send.at[k], recv_sem=tot_recv.at[k],
            device_id=(other // 2, lax.rem(other, 2)), device_id_type=MESH,
        )

    def tot_start(k, carry):
        tot_copy(k).start()
        return carry

    def tot_wait(k, carry):
        tot_copy(k).wait()
        return carry

    lax.fori_loop(1, devices, tot_start, 0)

    for copy in (src_pair, v_pair, m_pair, up_pair, dense_pair, low_pair, s_pair, w_pair):
        copy.wait_send()
    for copy in g1 + g3:
        copy.wait_send()
    when_each(lambda m: m < g, lambda copy: copy.wait_send(), off_copies)
    when_each(lambda m: jnp.logical_and(inner, m != g), lambda copy: copy.wait_send(), lin_copies)
    when_each(lambda m: m > g, lambda copy: copy.wait_send(), o_copies)

    @pl.when(i > 0)
    def _():
        v_hop.wait_send()
        up_hop.wait_send()

    @pl.when(i < rows - 1)
    def _():
        x_hop.wait_send()

    lax.fori_loop(1, devices, tot_wait, 0)
    sums = jnp.sum(tot_all[...], axis=0)
    locations = rows * size
    for k in range(params):
        for m in range(params):
            at = min(k, m) * params + max(k, m)
            fisher_ref[k:k + 1, m:m + 1] = sums[:, at:at + 1] / (2.0 * count * locations)
    at = params * params
    trace, data = sums[:, at:at + params], sums[:, at + params:at + 2 * params]
    score_ref[...] = (data - trace / count) / (2.0 * locations)


def body(
    inv_diag, low_left, low_right, deriv_diag, deriv_left, deriv_right, ranks, whitened, probes
):
    rows = lax.axis_size("row")
    _, size, half = inv_diag.shape
    rmax = low_left.shape[2]
    params = deriv_left.shape[0]
    count = probes.shape[0]
    pad = -(-(count + 1) // 8) * 8
    group = group_size(rows)
    groups = rows // group
    devices = 2 * rows
    lanes = -(-(params * params + 2 * params) // 128) * 128
    vm, dma = pltpu.VMEM, pltpu.SemaphoreType.DMA
    high = rmax + pad
    packed = -(-params * (count + 1) // 8) * 8
    outs = pl.pallas_call(
        functools.partial(kernel, rows),
        out_shape=(
            jax.ShapeDtypeStruct((count + 1, half), f32),
            jax.ShapeDtypeStruct((params, count, half), f32),
            jax.ShapeDtypeStruct((params, params), f32),
            jax.ShapeDtypeStruct((1, params), f32),
        ),
        in_specs=[pl.BlockSpec(memory_space=pltpu.HBM)] * 9,
        out_specs=[pl.BlockSpec(memory_space=pltpu.VMEM)] * 4,
        scratch_shapes=[
            vm((1, params + 1), jnp.int32), vm((half,), f32), vm((count, half), jnp.int32),
            vm((half, size), f32), vm((rmax, half), f32), vm((rmax, half), f32),
            vm((params, half, size), bf16), vm((params, rmax, half), f32),
            vm((params, rmax, half), f32), vm((half, size), bf16), vm((half, size), bf16),
            vm((2, rmax, half), f32), vm((2, pad, half), f32),
            vm((params, rmax, half), bf16), vm((params, rmax, half), bf16),
            vm((params, rmax, half), bf16), vm((params, rmax, half), bf16),
            vm((high, rmax), f32), vm((high, rmax), f32), vm((group, high, rmax), f32),
            vm((groups, rmax, rmax), f32), vm((groups, pad, rmax), f32),
            vm((pad, half), f32), vm((pad, half), f32),
            vm((params, pad, rmax), f32), vm((params, pad, rmax), f32),
            vm((packed, half), f32), vm((packed, half), f32),
            vm((packed, half), f32), vm((packed, half), f32),
            vm((params, pad, rmax), f32), vm((params, pad, rmax), f32),
            vm((params * count, rmax), f32), vm((params * count, rmax), f32),
            vm((group, params * count, rmax), f32), vm((groups, params * count, rmax), f32),
            vm((params * count, half), f32), vm((params * count, half), f32),
            vm((devices, 1, lanes), f32),
            dma((9,)), dma((8,)), dma((8,)), dma((3,)), dma((3,)),
            dma((group,)), dma((group,)), dma((groups,)), dma((groups,)), dma((groups,)), dma((groups,)),
            dma((group,)), dma((group,)), dma((groups,)), dma((groups,)),
            dma((devices,)), dma((devices,)),
        ],
        compiler_params=pltpu.CompilerParams(
            collective_id=0, has_side_effects=True, vmem_limit_bytes=60 * 1024 * 1024
        ),
    )(
        *[jnp.swapaxes(x, -1, -2) for x in (
            inv_diag, low_left, low_right, deriv_diag, deriv_left, deriv_right, ranks
        )],
        whitened, probes,
    )
    return outs[0], outs[1], outs[2], outs[3][0]


def solution(mesh):
    return jax.shard_map(
        body,
        mesh=mesh,
        in_specs=(
            P("row", None, "col"),
            P("row", "col", None),
            P("row", "col", None),
            P(None, "row", None, "col"),
            P(None, "row", "col", None),
            P(None, "row", "col", None),
            P(None, "row"),
            P(("row", "col")),
            P(None, ("row", "col")),
        ),
        out_specs=(P(None, ("row", "col")), P(None, None, ("row", "col")), P(), P()),
        check_vma=False,
    )
```

profile of v0, /device:TPU:0, one launch (start us, length us, event | category | flops | bytes accessed | tf_op | source)
XLA Modules:
  0.0 57.0 jit_solution(12158948921632634791)
XLA Ops:
  0.6 51.1 %shard_map.120 = (f32[9,544]{1,0:T(8,128)}, f32[3,8,544]{2,1,0:T(8,128)}, f32[3,3]{1,0:T(4,128)}, f32[1,3]{1,0:T(1,128)}) custom-call(f32[1,544,1088]{2,1,0:T(8,128)} %bitcast.9, f32[1,96,544]{2,1,0:T(8,128)} %bitcast.12, f32[1,96,544]{2,1,0:T(8,128)} %bitcast.13, bf16[3,1,544,1088]{3,2,1,0:T(8,128)(2,1)} %bitcast.8, f32[3,1,96,544]{3,2,1,0:T(8,128)} %bitcast.10, ...), custom_call_target="tpu_custom_call" | custom-call | tf_op jit(solution)/shard_map/pallas_call | solution.py:423
  51.7 1.4 %copy.17 = f32[9,544]{1,0:T(8,128)} copy(f32[9,544]{1,0:T(8,128)} %get-tuple-element.16) | data formatting | bytes 39168
  53.1 1.5 %copy.18 = f32[3,8,544]{2,1,0:T(8,128)} copy(f32[3,8,544]{2,1,0:T(8,128)} %get-tuple-element.17) | data formatting | bytes 104448
  54.6 1.2 %copy.19 = f32[3,3]{1,0:T(4,128)} copy(f32[3,3]{1,0:T(4,128)} %get-tuple-element.18) | data formatting | bytes 72
  55.8 1.2 %copy.20 = f32[3]{0:T(128)} copy(f32[3]{0:T(128)} %bitcast.15) | data formatting | bytes 24
where the time goes:
time: 57.3 us; the launch traced here: 57 us
  Pallas kernels  51.1 us (89%)
  local copies, waits for them, and re-layouts  5.28 us (9%)
  between operations  0.64 us (1%)
    pallas_call x1, Pallas kernels, body(): pl.pallas_call(functools.partial(kernel, rows), out_shape=(jax.ShapeDtype...  51.1 us
    unnamed x4, local copies, waits for them, and re-layouts  5.28 us

commit v1 on v0

--- a/solution.py
+++ b/solution.py
@@ -404,6 +404,15 @@
     score_ref[...] = (data - trace / count) / (2.0 * locations)
 
 
+def store(*refs):
+    sem = refs[-1]
+    copies = [pltpu.make_async_copy(refs[k], refs[k + 4], sem.at[k]) for k in range(4)]
+    for copy in copies:
+        copy.start()
+    for copy in copies:
+        copy.wait()
+
+
 def body(
     inv_diag, low_left, low_right, deriv_diag, deriv_left, deriv_right, ranks, whitened, probes
 ):
@@ -423,10 +432,8 @@
     outs = pl.pallas_call(
         functools.partial(kernel, rows),
         out_shape=(
-            jax.ShapeDtypeStruct((count + 1, half), f32),
-            jax.ShapeDtypeStruct((params, count, half), f32),
-            jax.ShapeDtypeStruct((params, params), f32),
-            jax.ShapeDtypeStruct((1, params), f32),
+            vm((count + 1, half), f32), vm((params, count, half), f32),
+            vm((params, params), f32), vm((1, params), f32),
         ),
         in_specs=[pl.BlockSpec(memory_space=pltpu.HBM)] * 9,
         out_specs=[pl.BlockSpec(memory_space=pltpu.VMEM)] * 4,
@@ -463,6 +470,13 @@
         )],
         whitened, probes,
     )
+    outs = pl.pallas_call(
+        store,
+        out_shape=tuple(jax.ShapeDtypeStruct(x.shape, x.dtype) for x in outs),
+        in_specs=[pl.BlockSpec(memory_space=pltpu.VMEM)] * 4,
+        out_specs=[pl.BlockSpec(memory_space=pltpu.HBM)] * 4,
+        scratch_shapes=[dma((4,))],
+    )(*[pltpu.with_memory_space_constraint(x, pltpu.VMEM) for x in outs])
     return outs[0], outs[1], outs[2], outs[3][0]
 
 

time: 57.3 us -> 52 us (0.908)
  local copies, waits for them, and re-layouts: 5.28 us -> 0 us
    unnamed x4 -> x0, local copies, waits for them, and re-layouts: 5.28 us -> none
    pallas_call x1 -> x2, Pallas kernels: 51.1 us -> 51.2 us  [the longest x1 50.5 us: body(): pl.pallas_call(functools.partial(kernel, rows), out_shape=(vm((count + 1,...]
where the time goes in v1:
time: 52 us; the launch traced here: 51.8 us
  Pallas kernels  51.2 us (98%)
  between operations  0.64 us (1%)
    pallas_call x1, Pallas kernels, body(): pl.pallas_call(functools.partial(kernel, rows), out_shape=(vm((count + 1,...  50.5 us

profile of v1, /device:TPU:0, one launch (start us, length us, event | category | flops | bytes accessed | tf_op | source)
XLA Modules:
  0.0 51.8 jit_solution(2264054359182742403)
XLA Ops:
  0.6 50.5 %shard_map.120 = (f32[9,544]{1,0:T(8,128)S(1)}, f32[3,8,544]{2,1,0:T(8,128)S(1)}, f32[3,3]{1,0:T(4,128)S(1)}, f32[1,3]{1,0:T(1,128)S(1)}) custom-call(f32[1,544,1088]{2,1,0:T(8,128)} %bitcast.9, f32[1,96,544]{2,1,0:T(8,128)} %bitcast.12, f32[1,96,544]{2,1,0:T(8,128)} %bitcast.13, bf16[3,1,544,1088]{3,2,1,0:T(8,128)(2,1)} %bitcast.8, ...), custom_call_target="tpu_custom_call" | custom-call | tf_op jit(solution)/shard_map/pallas_call | solution.py:432
  51.1 0.7 %shard_map.121 = (f32[9,544]{1,0:T(8,128)}, f32[3,8,544]{2,1,0:T(8,128)}, f32[3,3]{1,0:T(4,128)}, f32[1,3]{1,0:T(1,128)}) custom-call(f32[9,544]{1,0:T(8,128)S(1)} %get-tuple-element.12.refs_0_, f32[3,8,544]{2,1,0:T(8,128)S(1)} %get-tuple-element.13.refs_1_, f32[3,3]{1,0:T(4,128)S(1)} %get-tuple-element.14.refs_2_, f32[1,3]{1,0:T(1,128)S(1)} %get-tuple-element.15.refs_3_), custom_call_target="tpu_custom_call" | custom-call | tf_op jit(solution)/shard_map/pallas_call | solution.py:473

commit v2 on v1

--- a/solution.py
+++ b/solution.py
@@ -38,9 +38,9 @@
     rows, q_hbm, u_hbm, v_hbm, d_hbm, du_hbm, dv_hbm, ranks_hbm, white_hbm, probes_hbm,
     solved_ref, deriv_ref, fisher_ref, score_ref,
     ranks_ref, white_ref, probes_ref, q, u, own_v, d, du, dv, q_high, q_low, v_all, src_all,
-    du_high, du_low, dv_high, dv_low,
-    m_part, m_other, m_all, lin_all, off_all, x_own, x_prior, up_part, up_other, up_send, up_recv,
-    dense_send, dense_recv, low_part, low_other, s_part, s_other, s_all, o_all,
+    du_high, du_low, dv_high, dv_low, p_send, p_recv, p_high, p_low, wd_part, wd_other,
+    m_part, m_other, m_all, lin_all, off_all, x_own, x_prior, up_send, up_recv,
+    dense_own, dense_send, dense_recv, low_part, low_other, s_all, o_all,
     w_send, w_recv, tot_all,
     load_sem, pair_send, pair_recv, row_send, row_recv,
     g1_send, g1_recv, l_send, l_recv, g2_send, g2_recv, g3_send, g3_recv, g4_send, g4_recv, tot_send, tot_recv,
@@ -50,7 +50,7 @@
     half, size = q.shape
     rmax = u.shape[0]
     params = d.shape[0]
-    count = s_part.shape[0] // params
+    count = probes_ref.shape[0]
     pad = src_all.shape[1]
     group = m_all.shape[0]
     groups = lin_all.shape[0]
@@ -100,6 +100,10 @@
             device_id=(lax.rem(i + distance + rows, rows), c), device_id_type=MESH,
         )
 
+    def halves_of(block):
+        low, high = block[:, :half], block[:, half:]
+        return jnp.where(c == 0, low, high), jnp.where(c == 0, high, low)
+
     own_v_load.wait()
     v_hop = hop(0, own_v, v_all.at[c], -1)
 
@@ -117,16 +121,24 @@
     src_pair = pair(0, src_all.at[c], src_all.at[c])
     src_pair.start()
 
-    lane_of = lax.broadcasted_iota(jnp.int32, (1, rmax), 1)
     row_of = lax.broadcasted_iota(jnp.int32, (rmax, 1), 0)
-    masks = [(lane_of < ranks_ref[:, k:k + 1]).astype(f32) for k in range(params + 1)]
     loads[0].wait()
-    u[...] = u[...] * (row_of < ranks_ref[:, 0:1]).astype(f32)
-    u_split = split(u[...])
+    u_split = split(u[...] * (row_of < ranks_ref[:, 0:1]).astype(f32))
     loads[1].wait()
     q_high[...], q_low[...] = split(q[...])
-
-    v_pair = pair(1, v_all.at[c], v_all.at[c])
+    p_own, p_send[...] = halves_of(dot3(u_split, (q_high[...], q_low[...]), NN))
+    p_pair = pair(1, p_send, p_recv)
+    p_pair.start()
+    for load in loads[2:4]:
+        load.wait()
+    for k in range(params):
+        du_high[k], du_low[k] = split(du[k] * (row_of < ranks_ref[:, k + 1:k + 2]).astype(f32))
+        dv_high[k], dv_low[k] = split(dv[k])
+    p_pair.wait_recv()
+    p_high[...], p_low[...] = split(p_own + p_recv[...])
+    src_pair.wait_recv()
+
+    v_pair = pair(2, v_all.at[c], v_all.at[c])
 
     @pl.when(i < rows - 1)
     def _():
@@ -137,19 +149,12 @@
         v_all[c] = jnp.zeros((rmax, half), f32)
 
     v_pair.start()
-    src_pair.wait_recv()
-    v_pair.wait_recv()
-
-    halves = [jnp.concatenate([v_all[s], src_all[s]], axis=0) for s in range(2)]
-    both = dot3(split(jnp.concatenate(halves, axis=1)), (q_high[...], q_low[...]), NT)
-    wide_t, base = both[:rmax], both[rmax:]
-    wide_split = split(wide_t)
-    m_part[...] = dot3(split(both), u_split, NT)
-    m_pair = pair(2, m_part, m_other)
+    p_split = (p_high[...], p_low[...])
+    m_part[...] = dot3(split(jnp.concatenate([v_all[c], src_own], axis=0)), p_split, NT)
+    m_pair = pair(3, m_part, m_other)
     m_pair.start()
     m_pair.wait_recv()
-    m_own = m_part[...] + m_other[...]
-    m_all[l] = m_own
+    m_all[l] = m_part[...] + m_other[...]
 
     def spread(block, mine, send, recv, span, device):
         copies = []
@@ -167,19 +172,36 @@
     across = lambda other: other * group + l
 
     g1 = spread(m_all, l, g1_send, g1_recv, group, in_group)
-    for load in loads[2:4]:
-        load.wait()
-    for k in range(params):
-        du_high[k], du_low[k] = split(du[k])
-        dv_high[k], dv_low[k] = split(dv[k])
+
+    v_pair.wait_recv()
+    halves = [jnp.concatenate([v_all[s], src_all[s]], axis=0) for s in range(2)]
+    both = dot3(split(jnp.concatenate(halves, axis=1)), (q_high[...], q_low[...]), NT)
+    base = both[rmax:]
+    both_split = split(both)
+    wide_split = tuple(part[:rmax] for part in both_split)
+    du_split = [(du_high[k], du_low[k]) for k in range(params)]
+    dv_split = [(dv_high[k], dv_low[k]) for k in range(params)]
+    for k in range(params):
+        wd_part[k] = dot3(both_split, du_split[k], NT)
+    wd_pair = pair(4, wd_part, wd_other)
+    wd_pair.start()
+
     for copy in g1:
         copy.wait_recv()
     m_split = [split(m_all[m, :rmax]) for m in range(group)]
     lift = [m_all[m, rmax:] for m in range(group)]
     lin, off = -m_all[group - 1, :rmax], lift[group - 1]
+    own_lin, own_off = lin, off
+    lin_split = {group - 1: split(lin)}
     for m in reversed(range(group - 1)):
-        state = dot3(split(jnp.concatenate([lin, off], axis=0)), m_split[m], NN)
+        own_lin, own_off = jnp.where(l <= m, lin, own_lin), jnp.where(l <= m, off, own_off)
+        off_split = split(off)
+        state = dot3(
+            tuple(jnp.concatenate(part, axis=0) for part in zip(lin_split[m + 1], off_split)), m_split[m], NN
+        )
         lin, off = -state[:rmax], lift[m] - state[rmax:]
+        if m > 0:
+            lin_split[m] = split(lin)
     lin_all[g] = lin
     off_all[g] = off
 
@@ -212,6 +234,22 @@
     off_copies = to_groups(off_all, g2_send, g2_recv)
     when_each(lambda m: m < g, lambda copy: copy.start(), off_copies)
     when_each(lambda m: jnp.logical_and(inner, m != g), lambda copy: copy.start(), lin_copies)
+
+    own_lin_split = split(own_lin)
+    lead = -m_all[0, :rmax]
+    own_lead = lead
+    for m in range(1, group - 1):
+        lead = -dot3(m_split[m], split(lead), NN)
+        own_lead = jnp.where(l > m, lead, own_lead)
+    lead_split = split(own_lead)
+    wd_pair.wait_recv()
+    wd_split, ub, dvw_split = [], [], []
+    for k in range(params):
+        wd = wd_part[k] + wd_other[k]
+        wd_split.append(split(wd[:rmax]))
+        ub.append(wd[rmax:])
+        dvw_split.append(split(dot3(wd_split[k], dv_split[k], NN)))
+
     when_each(lambda m: m > g, lambda m: from_group(off_all, g2_recv, m).wait_recv(), everyone)
     for m in range(1, groups - 1):
         @pl.when(m != g)
@@ -224,45 +262,23 @@
         if m < groups - 1:
             new = new + dot3(split(a), t_split[m], NN)
         a = jnp.where(m > g, new, a)
-    for m in reversed(range(1, group)):
-        a = jnp.where(m > l, lift[m] - dot3(split(a), m_split[m], NN), a)
-
-    x = base - dot3(split(a), wide_split, NN)
+    a = jnp.where(l < group - 1, own_off + dot3(split(a), own_lin_split, NN), a)
+
+    a_split = split(a)
+    x = base - dot3(a_split, wide_split, NN)
     x_own[...] = x
     x_hop = hop(1, x_own, x_prior, 1)
 
     @pl.when(i < rows - 1)
     def _():
         x_hop.start()
-
-    x_split = split(x)
-    du_split = [(du_high[k], du_low[k]) for k in range(params)]
-    dv_split = [(dv_high[k], dv_low[k]) for k in range(params)]
-    for k in range(params):
-        up_part[k] = dot3(x_split, du_split[k], NT)
-    up_pair = pair(3, up_part, up_other)
-    up_pair.start()
-    solved_ref[0:1] = x[count:count + 1]
-    solved_ref[1:] = x[:count]
-    rounded = x_split[0]
-    loads[4].wait()
 
     def pack(ref, k, block):
         ref[k * count:(k + 1) * count] = block[:count]
         ref[params * count + k:params * count + k + 1] = block[count:count + 1]
 
-    def halves_of(block):
-        low, high = block[:, :half], block[:, half:]
-        return jnp.where(c == 0, low, high), jnp.where(c == 0, high, low)
-
-    dense = [halves_of(dot1(rounded, d[k], NN)) for k in range(params)]
-    for k in range(params):
-        pack(dense_send, k, dense[k][1])
-    dense_pair = pair(4, dense_send, dense_recv)
-    dense_pair.start()
-    up_pair.wait_recv()
-    for k in range(params):
-        coeff = (up_part[k] + up_other[k]) * masks[k + 1]
+    for k in range(params):
+        coeff = ub[k] - dot3(a_split, wd_split[k], NN)
         pack(up_send, k, dot3(split(coeff), dv_split[k], NN))
     up_hop = hop(2, up_send, up_recv, -1)
 
@@ -270,6 +286,17 @@
     def _():
         up_hop.start()
 
+    solved_ref[0:1] = x[count:count + 1]
+    solved_ref[1:] = x[:count]
+    rounded = x.astype(bf16)
+    loads[4].wait()
+    for k in range(params):
+        mine, theirs = halves_of(dot1(rounded, d[k], NN))
+        pack(dense_own, k, mine)
+        pack(dense_send, k, theirs)
+    dense_pair = pair(5, dense_send, dense_recv)
+    dense_pair.start()
+
     @pl.when(i > 0)
     def _():
         x_hop.wait_recv()
@@ -281,43 +308,58 @@
     prior_split = split(x_prior[...])
     for k in range(params):
         low_part[k] = dot3(prior_split, dv_split[k], NT)
-    low_pair = pair(5, low_part, low_other)
+    low_pair = pair(6, low_part, low_other)
     low_pair.start()
+    s_low = jnp.concatenate([dot3(prior_split, dvw_split[k], NT)[:count] for k in range(params)], axis=0)
+    dense_pair.wait_recv()
+
+    @pl.when(i < rows - 1)
+    def _():
+        up_hop.wait_recv()
+
+    @pl.when(i == rows - 1)
+    def _():
+        up_recv[...] = jnp.zeros(up_recv.shape, f32)
+
+    applied = dense_own[...] + dense_recv[...] + up_recv[...]
+    s_all[2 * l + c] = dot3(split(applied[:params * count]), wide_split, NT) + s_low
+    g3 = []
+    for k in range(group):
+        for other in range(2):
+            if k > 0 or other > 0:
+                g3.append(pltpu.make_async_remote_copy(
+                    src_ref=s_all.at[2 * l + c], dst_ref=s_all.at[2 * l + c],
+                    send_sem=g3_send.at[2 * k + other], recv_sem=g3_recv.at[2 * k + other],
+                    device_id=(in_group(lax.rem(l + k, group)), (c, p)[other]), device_id_type=MESH,
+                ))
+    for copy in g3:
+        copy.start()
+
     low_pair.wait_recv()
-    lower = []
-    for k in range(params):
-        coeff = (low_part[k] + low_other[k]) * masks[k + 1]
-        lower.append(dense[k][0] + dot3(split(coeff), du_split[k], NN))
-    dense_pair.wait_recv()
-
-    @pl.when(i < rows - 1)
-    def _():
-        up_hop.wait_recv()
-
-    @pl.when(i == rows - 1)
-    def _():
-        up_recv[...] = jnp.zeros(up_recv.shape, f32)
-
-    other = dense_recv[...] + up_recv[...]
-    drive = jnp.concatenate([part[:count] for part in lower], axis=0) + other[:params * count]
+    lower = [dot3(split(low_part[k] + low_other[k]), du_split[k], NN) for k in range(params)]
+    drive = applied[:params * count] + jnp.concatenate([block[:count] for block in lower], axis=0)
     observed = [
-        lower[k][count:count + 1] + other[params * count + k:params * count + k + 1]
-        for k in range(params)
+        applied[params * count + k:params * count + k + 1] + lower[k][count:count + 1] for k in range(params)
     ]
-    s_part[...] = dot3(split(drive), wide_split, NT)
-    s_pair = pair(6, s_part, s_other)
-    s_pair.start()
-    s_pair.wait_recv()
-    s_all[l] = s_part[...] + s_other[...]
-    g3 = spread(s_all, l, g3_send, g3_recv, group, in_group)
+    w, w_send[...] = halves_of(dot3(split(drive), (q_high[...], q_low[...]), NN))
+    w_pair = pair(7, w_send, w_recv)
+    w_pair.start()
+
     for copy in g3:
         copy.wait_recv()
-    total = s_all[0]
-    for m in range(1, group):
-        total = s_all[m] - dot3(split(total), m_split[m], NT)
+    s_sum = [s_all[2 * m] + s_all[2 * m + 1] for m in range(group)]
+    s_split = [split(s_sum[m]) for m in range(group - 1)]
+    total = s_sum[group - 1]
+    for m in range(group - 1):
+        total = total + dot3(s_split[m], lin_split[m + 1], NT)
     o_all[g] = total
     o_copies = to_groups(o_all, g4_send, g4_recv)
     when_each(lambda m: m > g, lambda copy: copy.start(), o_copies)
+    b = jnp.where(l > 0, s_sum[0], 0.0)
+    for m in range(1, group - 1):
+        b = jnp.where(m < l, s_sum[m] - dot3(split(b), m_split[m], NT), b)
+    w_pair.wait_recv()
+    w = w + w_recv[...] - dot3(split(b), p_split, NN)
     when_each(lambda m: m < g, lambda m: from_group(o_all, g4_recv, m).wait_recv(), everyone)
     b = jnp.zeros((params * count, rmax), f32)
     for m in range(groups - 1):
@@ -325,15 +367,9 @@
         if m > 0:
             new = new + dot3(split(b), t_split[m], NT)
         b = jnp.where(m < g, new, b)
-    for m in range(group - 1):
-        b = jnp.where(m < l, s_all[m] - dot3(split(b), m_split[m], NT), b)
-
-    rest = split(drive - dot3(split(b), u_split, NN))
-    w, w_send[...] = halves_of(dot3(rest, (q_high[...], q_low[...]), NN))
-    w_pair = pair(7, w_send, w_recv)
-    w_pair.start()
-    w_pair.wait_recv()
-    w = w + w_recv[...]
+    b = jnp.where(l > 0, dot3(split(b), lead_split, NT), b)
+
+    w = w - dot3(split(b), p_split, NN)
     parts = [w[k * count:(k + 1) * count] for k in range(params)]
     for k in range(params):
         deriv_ref[k] = parts[k]
@@ -375,7 +411,7 @@
 
     lax.fori_loop(1, devices, tot_start, 0)
 
-    for copy in (src_pair, v_pair, m_pair, up_pair, dense_pair, low_pair, s_pair, w_pair):
+    for copy in (src_pair, p_pair, v_pair, m_pair, wd_pair, dense_pair, low_pair, w_pair):
         copy.wait_send()
     for copy in g1 + g3:
         copy.wait_send()
@@ -445,20 +481,20 @@
             vm((2, rmax, half), f32), vm((2, pad, half), f32),
             vm((params, rmax, half), bf16), vm((params, rmax, half), bf16),
             vm((params, rmax, half), bf16), vm((params, rmax, half), bf16),
+            vm((rmax, half), f32), vm((rmax, half), f32), vm((rmax, half), bf16), vm((rmax, half), bf16),
+            vm((params, high, rmax), f32), vm((params, high, rmax), f32),
             vm((high, rmax), f32), vm((high, rmax), f32), vm((group, high, rmax), f32),
             vm((groups, rmax, rmax), f32), vm((groups, pad, rmax), f32),
             vm((pad, half), f32), vm((pad, half), f32),
+            vm((packed, half), f32), vm((packed, half), f32),
+            vm((packed, half), f32), vm((packed, half), f32), vm((packed, half), f32),
             vm((params, pad, rmax), f32), vm((params, pad, rmax), f32),
-            vm((packed, half), f32), vm((packed, half), f32),
-            vm((packed, half), f32), vm((packed, half), f32),
-            vm((params, pad, rmax), f32), vm((params, pad, rmax), f32),
-            vm((params * count, rmax), f32), vm((params * count, rmax), f32),
-            vm((group, params * count, rmax), f32), vm((groups, params * count, rmax), f32),
+            vm((2 * group, params * count, rmax), f32), vm((groups, params * count, rmax), f32),
             vm((params * count, half), f32), vm((params * count, half), f32),
             vm((devices, 1, lanes), f32),
             dma((9,)), dma((8,)), dma((8,)), dma((3,)), dma((3,)),
             dma((group,)), dma((group,)), dma((groups,)), dma((groups,)), dma((groups,)), dma((groups,)),
-            dma((group,)), dma((group,)), dma((groups,)), dma((groups,)),
+            dma((2 * group,)), dma((2 * group,)), dma((groups,)), dma((groups,)),
             dma((devices,)), dma((devices,)),
         ],
         compiler_params=pltpu.CompilerParams(

time: 52 us -> 46.3 us (0.89)
  Pallas kernels: 51.2 us -> 45.5 us
    pallas_call x1, Pallas kernels: 50.5 us -> 44.8 us  [body(): pl.pallas_call(functools.partial(kernel, rows), out_shape=(vm((count + 1,...]
where the time goes in v2:
time: 46.3 us; the launch traced here: 46.1 us
  Pallas kernels  45.5 us (98%)
  between operations  0.64 us (1%)
    pallas_call x1, Pallas kernels, body(): pl.pallas_call(functools.partial(kernel, rows), out_shape=(vm((count + 1,...  44.8 us

profile of v2, /device:TPU:0, one launch (start us, length us, event | category | flops | bytes accessed | tf_op | source)
XLA Modules:
  0.0 46.1 jit_solution(975752573874007849)
XLA Ops:
  0.6 44.8 %shard_map.120 = (f32[9,544]{1,0:T(8,128)S(1)}, f32[3,8,544]{2,1,0:T(8,128)S(1)}, f32[3,3]{1,0:T(4,128)S(1)}, f32[1,3]{1,0:T(1,128)S(1)}) custom-call(f32[1,544,1088]{2,1,0:T(8,128)} %bitcast.9, f32[1,96,544]{2,1,0:T(8,128)} %bitcast.12, f32[1,96,544]{2,1,0:T(8,128)} %bitcast.13, bf16[3,1,544,1088]{3,2,1,0:T(8,128)(2,1)} %bitcast.8, ...), custom_call_target="tpu_custom_call" | custom-call | tf_op jit(solution)/shard_map/pallas_call | solution.py:468
  45.5 0.7 %shard_map.121 = (f32[9,544]{1,0:T(8,128)}, f32[3,8,544]{2,1,0:T(8,128)}, f32[3,3]{1,0:T(4,128)}, f32[1,3]{1,0:T(1,128)}) custom-call(f32[9,544]{1,0:T(8,128)S(1)} %get-tuple-element.12.refs_0_, f32[3,8,544]{2,1,0:T(8,128)S(1)} %get-tuple-element.13.refs_1_, f32[3,3]{1,0:T(4,128)S(1)} %get-tuple-element.14.refs_2_, f32[1,3]{1,0:T(1,128)S(1)} %get-tuple-element.15.refs_3_), custom_call_target="tpu_custom_call" | custom-call | tf_op jit(solution)/shard_map/pallas_call | solution.py:509

commit v3 on v2

--- a/solution.py
+++ b/solution.py
@@ -39,7 +39,7 @@
     solved_ref, deriv_ref, fisher_ref, score_ref,
     ranks_ref, white_ref, probes_ref, q, u, own_v, d, du, dv, q_high, q_low, v_all, src_all,
     du_high, du_low, dv_high, dv_low, p_send, p_recv, p_high, p_low, wd_part, wd_other,
-    m_part, m_other, m_all, lin_all, off_all, x_own, x_prior, up_send, up_recv,
+    m_part, m_other, m_all, lin_all, lin_ahead, off_all, x_own, x_prior, up_send, up_recv,
     dense_own, dense_send, dense_recv, low_part, low_other, s_all, o_all,
     w_send, w_recv, tot_all,
     load_sem, pair_send, pair_recv, row_send, row_recv,
@@ -77,16 +77,27 @@
 
     barrier = pltpu.get_barrier_semaphore()
 
-    def greet(k, carry):
-        row = lax.rem(i + k, rows)
-        for col in range(2):
-            @pl.when(jnp.logical_or(k > 0, col != c))
-            def _():
-                pl.semaphore_signal(barrier, inc=1, device_id=(row, col), device_id_type=MESH)
-        return carry
-
-    lax.fori_loop(0, rows, greet, 0)
-    pl.semaphore_wait(barrier, 2 * rows - 1)
+    def greet(row, col):
+        pl.semaphore_signal(barrier, inc=1, device_id=(row, col), device_id_type=MESH)
+
+    from_above, to_below = jnp.logical_and(l == 0, i > 0), jnp.logical_and(l == group - 1, i < rows - 1)
+    greet(i, p)
+    for k in range(1, group):
+        greet(g * group + lax.rem(l + k, group), c)
+
+    @pl.when(from_above)
+    def _():
+        greet(i - 1, c)
+
+    @pl.when(to_below)
+    def _():
+        greet(i + 1, c)
+
+    for k in range(1, groups):
+        greet(lax.rem(g + k, groups) * group + l, c)
+    pl.semaphore_wait(
+        barrier, group + groups - 1 + from_above.astype(jnp.int32) + to_below.astype(jnp.int32)
+    )
 
     def pair(k, src, dst):
         return pltpu.make_async_remote_copy(
@@ -94,9 +105,9 @@
             device_id=(i, p), device_id_type=MESH,
         )
 
-    def hop(k, src, dst, distance):
+    def hop(sent, k, src, dst, distance):
         return pltpu.make_async_remote_copy(
-            src_ref=src, dst_ref=dst, send_sem=row_send.at[k], recv_sem=row_recv.at[k],
+            src_ref=src, dst_ref=dst, send_sem=row_send.at[sent], recv_sem=row_recv.at[k],
             device_id=(lax.rem(i + distance + rows, rows), c), device_id_type=MESH,
         )
 
@@ -105,7 +116,7 @@
         return jnp.where(c == 0, low, high), jnp.where(c == 0, high, low)
 
     own_v_load.wait()
-    v_hop = hop(0, own_v, v_all.at[c], -1)
+    v_hop = hop(0, 0, own_v, v_all.at[c], -1)
 
     @pl.when(i > 0)
     def _():
@@ -156,22 +167,18 @@
     m_pair.wait_recv()
     m_all[l] = m_part[...] + m_other[...]
 
-    def spread(block, mine, send, recv, span, device):
-        copies = []
-        for k in range(1, span):
-            copies.append(pltpu.make_async_remote_copy(
-                src_ref=block.at[mine], dst_ref=block.at[mine],
-                send_sem=send.at[k], recv_sem=recv.at[k],
-                device_id=(device(lax.rem(mine + k, span)), c), device_id_type=MESH,
-            ))
-        for copy in copies:
-            copy.start()
-        return copies
+    def drain(block, number, sem):
+        blocks = block.at[pl.ds(0, number)]
+        pltpu.make_async_copy(blocks, blocks, sem).wait()
 
     in_group = lambda member: g * group + member
     across = lambda other: other * group + l
 
-    g1 = spread(m_all, l, g1_send, g1_recv, group, in_group)
+    for k in range(1, group):
+        pltpu.make_async_remote_copy(
+            src_ref=m_all.at[l], dst_ref=m_all.at[l], send_sem=g1_send.at[0], recv_sem=g1_recv.at[0],
+            device_id=(in_group(lax.rem(l + k, group)), c), device_id_type=MESH,
+        ).start()
 
     v_pair.wait_recv()
     halves = [jnp.concatenate([v_all[s], src_all[s]], axis=0) for s in range(2)]
@@ -186,8 +193,7 @@
     wd_pair = pair(4, wd_part, wd_other)
     wd_pair.start()
 
-    for copy in g1:
-        copy.wait_recv()
+    drain(m_all, group - 1, g1_recv.at[0])
     m_split = [split(m_all[m, :rmax]) for m in range(group)]
     lift = [m_all[m, rmax:] for m in range(group)]
     lin, off = -m_all[group - 1, :rmax], lift[group - 1]
@@ -205,10 +211,10 @@
     lin_all[g] = lin
     off_all[g] = off
 
-    def to_groups(block, send, recv):
+    def to_groups(block, send, recv, into):
         return [
             pltpu.make_async_remote_copy(
-                src_ref=block.at[g], dst_ref=block.at[g],
+                src_ref=block.at[g], dst_ref=into.at[g],
                 send_sem=send.at[m], recv_sem=recv.at[g],
                 device_id=(across(m), c), device_id_type=MESH,
             )
@@ -230,10 +236,12 @@
 
     everyone = list(range(groups))
     inner = jnp.logical_and(g > 0, g < groups - 1)
-    lin_copies = to_groups(lin_all, l_send, l_recv)
-    off_copies = to_groups(off_all, g2_send, g2_recv)
+    lin_back = to_groups(lin_all, l_send, l_recv, lin_all)
+    lin_on = to_groups(lin_all, l_send, l_recv, lin_ahead)
+    off_copies = to_groups(off_all, g2_send, g2_recv, off_all)
     when_each(lambda m: m < g, lambda copy: copy.start(), off_copies)
-    when_each(lambda m: jnp.logical_and(inner, m != g), lambda copy: copy.start(), lin_copies)
+    when_each(lambda m: jnp.logical_and(inner, m < g), lambda copy: copy.start(), lin_back)
+    when_each(lambda m: jnp.logical_and(inner, m > g), lambda copy: copy.start(), lin_on)
 
     own_lin_split = split(own_lin)
     lead = -m_all[0, :rmax]
@@ -243,18 +251,16 @@
         own_lead = jnp.where(l > m, lead, own_lead)
     lead_split = split(own_lead)
     wd_pair.wait_recv()
-    wd_split, ub, dvw_split = [], [], []
+    up_base, dvw_split = [], []
     for k in range(params):
         wd = wd_part[k] + wd_other[k]
-        wd_split.append(split(wd[:rmax]))
-        ub.append(wd[rmax:])
-        dvw_split.append(split(dot3(wd_split[k], dv_split[k], NN)))
-
+        expanded = dot3(split(wd), dv_split[k], NN)
+        dvw_split.append(split(expanded[:rmax]))
+        up_base.append(expanded[rmax:])
+
+    maps = everyone[1:groups - 1]
     when_each(lambda m: m > g, lambda m: from_group(off_all, g2_recv, m).wait_recv(), everyone)
-    for m in range(1, groups - 1):
-        @pl.when(m != g)
-        def _():
-            from_group(lin_all, l_recv, m).wait_recv()
+    when_each(lambda k: maps[k] > g, lambda m: from_group(lin_all, l_recv, m).wait_recv(), maps)
     t_split = [split(lin_all[m]) for m in range(groups)]
     a = jnp.zeros((pad, rmax), f32)
     for m in reversed(range(1, groups)):
@@ -267,24 +273,33 @@
     a_split = split(a)
     x = base - dot3(a_split, wide_split, NN)
     x_own[...] = x
-    x_hop = hop(1, x_own, x_prior, 1)
-
-    @pl.when(i < rows - 1)
-    def _():
-        x_hop.start()
+
+    def pieces(sent, first, src, dst, distance):
+        return [
+            hop(sent, first + k, src.at[pl.ds(k * 8, 8)], dst.at[pl.ds(k * 8, 8)], distance)
+            for k in range(src.shape[0] // 8)
+        ]
+
+    x_hops = pieces(1, 1, x_own, x_prior, 1)
+    up_hops = pieces(2, 1 + pad // 8, up_send, up_recv, -1)
+
+    def start_when(test, copies):
+        @pl.when(test)
+        def _():
+            for copy in copies:
+                copy.start()
+
+    start_when(i < rows - 1, x_hops[:count // 8])
 
     def pack(ref, k, block):
         ref[k * count:(k + 1) * count] = block[:count]
         ref[params * count + k:params * count + k + 1] = block[count:count + 1]
 
     for k in range(params):
-        coeff = ub[k] - dot3(a_split, wd_split[k], NN)
-        pack(up_send, k, dot3(split(coeff), dv_split[k], NN))
-    up_hop = hop(2, up_send, up_recv, -1)
-
-    @pl.when(i > 0)
-    def _():
-        up_hop.start()
+        pack(up_send, k, up_base[k] - dot3(a_split, dvw_split[k], NN))
+        start_when(i > 0, up_hops[k * count // 8:(k + 1) * count // 8])
+    start_when(i < rows - 1, x_hops[count // 8:])
+    start_when(i > 0, up_hops[params * count // 8:])
 
     solved_ref[0:1] = x[count:count + 1]
     solved_ref[1:] = x[:count]
@@ -297,75 +312,74 @@
     dense_pair = pair(5, dense_send, dense_recv)
     dense_pair.start()
 
-    @pl.when(i > 0)
-    def _():
-        x_hop.wait_recv()
-
-    @pl.when(i == 0)
-    def _():
-        x_prior[...] = jnp.zeros((pad, half), f32)
-
+    def wait_or_clear(test, copies, rows_of):
+        @pl.when(test)
+        def _():
+            for copy in copies:
+                copy.wait_recv()
+
+        @pl.when(jnp.logical_not(test))
+        def _():
+            rows_of[...] = jnp.zeros(rows_of.shape, f32)
+
+    wait_or_clear(i > 0, x_hops[:count // 8], x_prior.at[pl.ds(0, count)])
+    signs_split = split(x_prior[:count])
+    s_low = jnp.concatenate([dot3(signs_split, dvw_split[k], NT) for k in range(params)], axis=0)
+    dense_pair.wait_recv()
+    probe_rows = params * count
+    wait_or_clear(i < rows - 1, up_hops[:probe_rows // 8], up_recv.at[pl.ds(0, probe_rows)])
+
+    applied = dense_own[:probe_rows] + dense_recv[:probe_rows] + up_recv[:probe_rows]
+    s_all[2 * l + c] = dot3(split(applied), wide_split, NT) + s_low
+    for k in range(group):
+        for other in range(2):
+            if k > 0 or other > 0:
+                pltpu.make_async_remote_copy(
+                    src_ref=s_all.at[2 * l + c], dst_ref=s_all.at[2 * l + c],
+                    send_sem=g3_send.at[0], recv_sem=g3_recv.at[0],
+                    device_id=(in_group(lax.rem(l + k, group)), (c, p)[other]), device_id_type=MESH,
+                ).start()
+
+    rest = x_prior.shape[0] - count
+    wait_or_clear(i > 0, x_hops[count // 8:], x_prior.at[pl.ds(count, rest)])
     prior_split = split(x_prior[...])
     for k in range(params):
         low_part[k] = dot3(prior_split, dv_split[k], NT)
     low_pair = pair(6, low_part, low_other)
     low_pair.start()
-    s_low = jnp.concatenate([dot3(prior_split, dvw_split[k], NT)[:count] for k in range(params)], axis=0)
-    dense_pair.wait_recv()
-
-    @pl.when(i < rows - 1)
-    def _():
-        up_hop.wait_recv()
-
-    @pl.when(i == rows - 1)
-    def _():
-        up_recv[...] = jnp.zeros(up_recv.shape, f32)
-
-    applied = dense_own[...] + dense_recv[...] + up_recv[...]
-    s_all[2 * l + c] = dot3(split(applied[:params * count]), wide_split, NT) + s_low
-    g3 = []
-    for k in range(group):
-        for other in range(2):
-            if k > 0 or other > 0:
-                g3.append(pltpu.make_async_remote_copy(
-                    src_ref=s_all.at[2 * l + c], dst_ref=s_all.at[2 * l + c],
-                    send_sem=g3_send.at[2 * k + other], recv_sem=g3_recv.at[2 * k + other],
-                    device_id=(in_group(lax.rem(l + k, group)), (c, p)[other]), device_id_type=MESH,
-                ))
-    for copy in g3:
-        copy.start()
-
+    rest = up_recv.shape[0] - probe_rows
+    wait_or_clear(i < rows - 1, up_hops[probe_rows // 8:], up_recv.at[pl.ds(probe_rows, rest)])
     low_pair.wait_recv()
     lower = [dot3(split(low_part[k] + low_other[k]), du_split[k], NN) for k in range(params)]
-    drive = applied[:params * count] + jnp.concatenate([block[:count] for block in lower], axis=0)
-    observed = [
-        applied[params * count + k:params * count + k + 1] + lower[k][count:count + 1] for k in range(params)
-    ]
+    drive = applied + jnp.concatenate([block[:count] for block in lower], axis=0)
+    white_rows = pl.ds(probe_rows, params)
+    seen = dense_own[white_rows] + dense_recv[white_rows] + up_recv[white_rows]
+    observed = [seen[k:k + 1] + lower[k][count:count + 1] for k in range(params)]
     w, w_send[...] = halves_of(dot3(split(drive), (q_high[...], q_low[...]), NN))
     w_pair = pair(7, w_send, w_recv)
     w_pair.start()
 
-    for copy in g3:
-        copy.wait_recv()
+    drain(s_all, 2 * group - 1, g3_recv.at[0])
     s_sum = [s_all[2 * m] + s_all[2 * m + 1] for m in range(group)]
     s_split = [split(s_sum[m]) for m in range(group - 1)]
     total = s_sum[group - 1]
     for m in range(group - 1):
         total = total + dot3(s_split[m], lin_split[m + 1], NT)
     o_all[g] = total
-    o_copies = to_groups(o_all, g4_send, g4_recv)
+    o_copies = to_groups(o_all, g4_send, g4_recv, o_all)
     when_each(lambda m: m > g, lambda copy: copy.start(), o_copies)
     b = jnp.where(l > 0, s_sum[0], 0.0)
     for m in range(1, group - 1):
         b = jnp.where(m < l, s_sum[m] - dot3(split(b), m_split[m], NT), b)
     w_pair.wait_recv()
     w = w + w_recv[...] - dot3(split(b), p_split, NN)
+    when_each(lambda k: maps[k] < g, lambda m: from_group(lin_ahead, l_recv, m).wait_recv(), maps)
     when_each(lambda m: m < g, lambda m: from_group(o_all, g4_recv, m).wait_recv(), everyone)
     b = jnp.zeros((params * count, rmax), f32)
     for m in range(groups - 1):
         new = o_all[m]
         if m > 0:
-            new = new + dot3(split(b), t_split[m], NT)
+            new = new + dot3(split(b), split(lin_ahead[m]), NT)
         b = jnp.where(m < g, new, b)
     b = jnp.where(l > 0, dot3(split(b), lead_split, NT), b)
 
@@ -393,42 +407,35 @@
     devices = 2 * rows
     tot_all[me] = packed
 
-    def tot_copy(k):
+    def tot_start(k, carry):
         other = lax.rem(me + k, devices)
-        return pltpu.make_async_remote_copy(
-            src_ref=tot_all.at[me], dst_ref=tot_all.at[me],
-            send_sem=tot_send.at[k], recv_sem=tot_recv.at[k],
+        pltpu.make_async_remote_copy(
+            src_ref=tot_all.at[me], dst_ref=tot_all.at[me], send_sem=tot_send.at[0], recv_sem=tot_recv.at[0],
             device_id=(other // 2, lax.rem(other, 2)), device_id_type=MESH,
-        )
-
-    def tot_start(k, carry):
-        tot_copy(k).start()
+        ).start()
         return carry
 
-    def tot_wait(k, carry):
-        tot_copy(k).wait()
-        return carry
-
-    lax.fori_loop(1, devices, tot_start, 0)
+    lax.fori_loop(1, devices, tot_start, 0, unroll=min(devices - 1, 31))
 
     for copy in (src_pair, p_pair, v_pair, m_pair, wd_pair, dense_pair, low_pair, w_pair):
         copy.wait_send()
-    for copy in g1 + g3:
-        copy.wait_send()
+    drain(m_all, group - 1, g1_send.at[0])
+    drain(s_all, 2 * group - 1, g3_send.at[0])
     when_each(lambda m: m < g, lambda copy: copy.wait_send(), off_copies)
-    when_each(lambda m: jnp.logical_and(inner, m != g), lambda copy: copy.wait_send(), lin_copies)
+    when_each(lambda m: jnp.logical_and(inner, m != g), lambda copy: copy.wait_send(), lin_back)
     when_each(lambda m: m > g, lambda copy: copy.wait_send(), o_copies)
 
     @pl.when(i > 0)
     def _():
         v_hop.wait_send()
-        up_hop.wait_send()
+        hop(2, 0, up_send, up_recv, -1).wait_send()
 
     @pl.when(i < rows - 1)
     def _():
-        x_hop.wait_send()
-
-    lax.fori_loop(1, devices, tot_wait, 0)
+        hop(1, 0, x_own, x_prior, 1).wait_send()
+
+    drain(tot_all, devices - 1, tot_send.at[0])
+    drain(tot_all, devices - 1, tot_recv.at[0])
     sums = jnp.sum(tot_all[...], axis=0)
     locations = rows * size
     for k in range(params):
@@ -465,6 +472,7 @@
     vm, dma = pltpu.VMEM, pltpu.SemaphoreType.DMA
     high = rmax + pad
     packed = -(-params * (count + 1) // 8) * 8
+    hops = 1 + pad // 8 + packed // 8
     outs = pl.pallas_call(
         functools.partial(kernel, rows),
         out_shape=(
@@ -484,7 +492,7 @@
             vm((rmax, half), f32), vm((rmax, half), f32), vm((rmax, half), bf16), vm((rmax, half), bf16),
             vm((params, high, rmax), f32), vm((params, high, rmax), f32),
             vm((high, rmax), f32), vm((high, rmax), f32), vm((group, high, rmax), f32),
-            vm((groups, rmax, rmax), f32), vm((groups, pad, rmax), f32),
+            vm((groups, rmax, rmax), f32), vm((groups, rmax, rmax), f32), vm((groups, pad, rmax), f32),
             vm((pad, half), f32), vm((pad, half), f32),
             vm((packed, half), f32), vm((packed, half), f32),
             vm((packed, half), f32), vm((packed, half), f32), vm((packed, half), f32),
@@ -492,10 +500,10 @@
             vm((2 * group, params * count, rmax), f32), vm((groups, params * count, rmax), f32),
             vm((params * count, half), f32), vm((params * count, half), f32),
             vm((devices, 1, lanes), f32),
-            dma((9,)), dma((8,)), dma((8,)), dma((3,)), dma((3,)),
-            dma((group,)), dma((group,)), dma((groups,)), dma((groups,)), dma((groups,)), dma((groups,)),
-            dma((2 * group,)), dma((2 * group,)), dma((groups,)), dma((groups,)),
-            dma((devices,)), dma((devices,)),
+            dma((9,)), dma((8,)), dma((8,)), dma((3,)), dma((hops,)),
+            dma((1,)), dma((1,)), dma((groups,)), dma((groups,)), dma((groups,)), dma((groups,)),
+            dma((1,)), dma((1,)), dma((groups,)), dma((groups,)),
+            dma((1,)), dma((1,)),
         ],
         compiler_params=pltpu.CompilerParams(
             collective_id=0, has_side_effects=True, vmem_limit_bytes=60 * 1024 * 1024

time: 46.3 us -> 43.2 us (0.933)
  Pallas kernels: 45.5 us -> 42.4 us
    pallas_call x1, Pallas kernels: 44.8 us -> 41.7 us  [body(): pl.pallas_call(functools.partial(kernel, rows), out_shape=(vm((count + 1,...]
where the time goes in v3:
time: 43.2 us; the launch traced here: 43 us
  Pallas kernels  42.4 us (98%)
  between operations  0.64 us (1%)
    pallas_call x1, Pallas kernels, body(): pl.pallas_call(functools.partial(kernel, rows), out_shape=(vm((count + 1,...  41.7 us

profile of v3, /device:TPU:0, one launch (start us, length us, event | category | flops | bytes accessed | tf_op | source)
XLA Modules:
  0.0 43.0 jit_solution(14579951011538508849)
XLA Ops:
  0.6 41.7 %shard_map.120 = (f32[9,544]{1,0:T(8,128)S(1)}, f32[3,8,544]{2,1,0:T(8,128)S(1)}, f32[3,3]{1,0:T(4,128)S(1)}, f32[1,3]{1,0:T(1,128)S(1)}) custom-call(f32[1,544,1088]{2,1,0:T(8,128)} %bitcast.9, f32[1,96,544]{2,1,0:T(8,128)} %bitcast.12, f32[1,96,544]{2,1,0:T(8,128)} %bitcast.13, bf16[3,1,544,1088]{3,2,1,0:T(8,128)(2,1)} %bitcast.8, ...), custom_call_target="tpu_custom_call" | custom-call | tf_op jit(solution)/shard_map/pallas_call | solution.py:476
  42.3 0.7 %shard_map.121 = (f32[9,544]{1,0:T(8,128)}, f32[3,8,544]{2,1,0:T(8,128)}, f32[3,3]{1,0:T(4,128)}, f32[1,3]{1,0:T(1,128)}) custom-call(f32[9,544]{1,0:T(8,128)S(1)} %get-tuple-element.12.refs_0_, f32[3,8,544]{2,1,0:T(8,128)S(1)} %get-tuple-element.13.refs_1_, f32[3,3]{1,0:T(4,128)S(1)} %get-tuple-element.14.refs_2_, f32[1,3]{1,0:T(1,128)S(1)} %get-tuple-element.15.refs_3_), custom_call_target="tpu_custom_call" | custom-call | tf_op jit(solution)/shard_map/pallas_call | solution.py:517
